TPU v7x, 256 devices: a whole 4x4x8 slice. The times are simulated.
256 devices in a mesh: section: 8 (over z), col: 32 (over y, x, core).
Axes of the slice: x: 4, y: 4, z: 8, core: 2. Of those that a mesh axis runs over, the one named last changes fastest.
Arguments:
- tiles: bfloat16 [1024, 12, 128, 128], P('col', None, 'section'), may hold values from 0.0099487305 to 1
- offsets: int32 [1024, 12], replicated, may hold values from -6 to 6, as said below
- counts: int32 [1024], replicated, may hold values from 1 to 12
- ranks: int32 [1024, 25, 128, 128], P('col', None, 'section'), may hold values from 0 to 3199, as said below
Outputs:
- pruned: bfloat16 [1024, 25, 128, 128], P('col', None, 'section')
Inputs may be any that keep to these rules, and one draw needn't show every extreme that they name: Within each panel the 12 offsets are distinct, each from -6 to 6. For every panel j and column c, ranks[j, :, c, :] holds each of 0 .. 3199 once.
All inputs are finite; a program needn't handle non-finite values.
Results may differ from a plain program's by a relative error of at most 0.001.
Values may be sent and summed in bfloat16 or wider, within the bound.
A program may use at most 128 MiB of HBM per device.

v0:
```python
import jax
import jax.numpy as jnp
from jax import lax
from jax.sharding import PartitionSpec as P

W = 6
TOPK = 256


def extended(shard, sides, width):
    for axis, dim in sides:
        count, length = (lax.axis_size(axis), shard.shape[dim])
        up = [(i, (i + 1) % count) for i in range(count - 1)]
        down = [(j, i) for i, j in up]
        last = lax.slice_in_dim(shard, length - width, length, axis=dim)
        initial = lax.slice_in_dim(shard, 0, width, axis=dim)
        before = lax.ppermute(last, axis, up)
        after = lax.ppermute(initial, axis, down)
        shard = jnp.concatenate([before, shard, after], axis=dim)
    return shard


def cut_along(shard, dim, count):
    before, after = (shard.shape[:dim], shard.shape[dim + 1 :])
    return jnp.moveaxis(shard.reshape(*before, count, -1, *after), dim, 0)


def piece_ends(length, count):
    unit = 8 if length >= 8 * count else 1
    return [length // unit * k // count * unit for k in range(1, count)]


def joined_along(tiles, dim):
    tiles = jnp.moveaxis(tiles, 0, dim)
    dims = tiles.shape
    return tiles.reshape(*dims[:dim], dims[dim] * dims[dim + 1], *dims[dim + 2 :])


def exchange_in_pieces(shard, axis, pieces, split_dim, concat_dim):
    tiles = cut_along(shard, split_dim, lax.axis_size(axis))
    split_at = max(range(1, max(2, tiles.ndim - 1)), key=lambda d: tiles.shape[d])
    outs = []
    for share in jnp.split(tiles, piece_ends(tiles.shape[split_at], pieces), axis=split_at):
        if share.size:
            outs.append(lax.all_to_all(share, axis, split_axis=0, concat_axis=0, tiled=True))
    return joined_along(jnp.concatenate(outs, axis=split_at), concat_dim)


def expand(own, own_off, own_cnt, center, global_panel, banded, band_off, band_cnt, total, bands):
    slots = own.shape[0]
    slot_ids = jnp.arange(slots, dtype=jnp.int32)
    where_at = center + W + own_off
    firsts = banded[where_at]
    first_off = band_off[where_at]
    first_cnt = band_cnt[where_at]
    row_own = global_panel + own_off
    ok_own = (slot_ids < own_cnt) & (row_own >= 0) & (row_own < total)
    row_first = row_own[:, None] + first_off
    ok_first = (slot_ids[None, :] < first_cnt[:, None]) & (row_first >= 0) & (row_first < total)
    weight = (ok_own[:, None] & ok_first).astype(jnp.float32)
    target = own_off[:, None] + first_off + 2 * W
    products = jnp.einsum("kcx,klxr->klcr", own, firsts, preferred_element_type=jnp.float32)
    weighted = products * weight[:, :, None, None]
    columns = own.shape[1]
    rows = own.shape[2]
    empty = jnp.zeros((bands, columns, rows), jnp.float32)
    return empty.at[target.reshape(-1)].add(weighted.reshape((slots * slots, columns, rows)))


def finish(expanded, rank_block):
    keep = rank_block < TOPK
    squared = jnp.where(keep, expanded * expanded, jnp.float32(0.0))
    totals = jnp.sum(squared, axis=(0, 2), keepdims=True)
    return (TOPK * squared / (totals + 1e-06)).astype(jnp.bfloat16)


def shards(tiles, offsets, counts, ranks):
    panels = tiles.shape[0]
    slots = tiles.shape[1]
    bands = ranks.shape[1]
    total = offsets.shape[0]
    first_panel = lax.axis_index("col") * panels
    pad_off = jnp.concatenate(
        [jnp.zeros((W, slots), jnp.int32), offsets, jnp.zeros((W, slots), jnp.int32)], axis=0
    )
    pad_cnt = jnp.concatenate(
        [jnp.zeros((W,), jnp.int32), counts, jnp.zeros((W,), jnp.int32)], axis=0
    )
    sections = lax.axis_size("section")
    share = panels // sections
    start = first_panel + lax.axis_index("section") * share
    sliced = extended(tiles, (("col", 0),), W)
    windows = jnp.stack([sliced[t * share : t * share + share + 2 * W] for t in range(sections)], 0)
    whole = lax.all_to_all(windows, "section", split_axis=0, concat_axis=3, tiled=True)[0]
    win_off = lax.dynamic_slice_in_dim(pad_off, start, share + 2 * W, 0)
    win_cnt = lax.dynamic_slice_in_dim(pad_cnt, start, share + 2 * W, 0)
    loc_off = lax.dynamic_slice_in_dim(offsets, start, share, 0)
    loc_cnt = lax.dynamic_slice_in_dim(counts, start, share, 0)

    def one_whole(packed):
        p_off, p_cnt, centre = packed
        own = lax.dynamic_index_in_dim(whole, centre + W, 0, False)
        return expand(
            own, p_off, p_cnt, centre, start + centre, whole, win_off, win_cnt, total, bands
        )

    expanded = lax.map(one_whole, (loc_off, loc_cnt, jnp.arange(share, dtype=jnp.int32)))
    back = exchange_in_pieces(expanded, "section", 2, 2, 0)

    def one_finish(packed):
        values, rank_block = packed
        return finish(values, rank_block)

    return lax.map(one_finish, (back, ranks))


def solution(mesh):
    placed = (P("col", None, "section", None), P(), P(), P("col", None, "section", None))
    return jax.shard_map(
        shards,
        mesh=mesh,
        in_specs=placed,
        out_specs=P("col", None, "section", None),
        check_vma=False,
    )
```

profile of v0, /device:TPU:14, one launch (start us, length us, event | category | flops | bytes accessed | tf_op | source)
XLA Modules:
  0.0 642.6 jit_solution(12305052271781320024)
XLA Ops:
  1.3 1.9 collective-permute-start
  3.2 3.6 collective-permute-start.1
  6.9 2.5 collective-permute-done
  19.7 8.6 %all-to-all-start = ((bf16[8,16,12,16,128]{4,3,2,1,0:T(8,128)(2,1)}), bf16[8,16,12,16,128]{4,3,2,1,0:T(8,128)(2,1)}, u32[]{:S(2)}, u32[]{:S(2)}) async-start(bf16[8,16,12,16,128]{4,3,2,1,0:T(8,128)(2,1)} %fusion.11), calls=%async_computation | async-start | bytes 12582912 | tf_op jit(solution)/shard_map/all_to_all | solution.py:94
  29.0 140.1 %all-to-all-done = bf16[8,16,12,16,128]{4,3,2,1,0:T(8,128)(2,1)} async-done(((bf16[8,16,12,16,128]{4,3,2,1,0:T(8,128)(2,1)}), bf16[8,16,12,16,128]{4,3,2,1,0:T(8,128)(2,1)}, u32[]{:S(2)}, u32[]{:S(2)}) %all-to-all-start) | async-done | bytes 6291488 | tf_op jit(solution)/shard_map/all_to_all | solution.py:94
  169.1 7.3 %copy.20 = bf16[1,16,12,8,16,128]{5,4,3,2,1,0:T(8,128)(2,1)} copy(bf16[1,16,12,8,16,128]{5,4,2,1,3,0:T(8,128)(2,1)} %bitcast.21) | data formatting | bytes 12582912 | tf_op jit(solution)/shard_map/all_to_all | solution.py:94
  176.4 199.5 %while.22 = (s32[]{:T(128)}, f32[4,25,128,128]{3,2,1,0:T(8,128)}, s32[4,12]{1,0:T(4,128)S(1)}, s32[4]{0:T(128)S(1)}, s32[16,12]{1,0:T(8,128)S(1)}, /*index=5*/bf...) while((s32[]{:T(128)}, f32[4,25,128,128]{3,2,1,0:T(8,128)}, ...), condition=%wide.region_2.3_spmd, body=%wide.region_0.2_spmd.sunk | while | flops 608701376 | bytes 76102056 | solution.py:107
  181.4 6.3 gather_fusion.2
  187.7 8.0 %broadcast_multiply_fusion.2 = f32[12,12,128,128]{3,2,1,0:T(8,128)} fusion(f32[12,12]{1,0:T(8,128)S(1)} %fusion.27, bf16[12,12,128,128]{3,2,1,0:T(8,128)(2,1)} %gather_fusion.2, bf16[16,12,128,128]{3,2,1,0:T(8,128)(2,1)} %get-tuple-element.310, s32[]{:T(128)S(6)} %select_n.67), kind=kOutput, calls=%fused_computation.10.clone.1 | convolution fusion | flops 606339072 | bytes 14549572 | tf_op jit(solution)/shard_map/while/body/eval_jaxpr/kcx,klxr->klcr/dot_general | solution.py:62
  195.8 9.6 %copy.29 = f32[144,128,128]{2,1,0:T(8,128)} copy(f32[144,128,128]{1,2,0:T(8,128)} %bitcast.73) | data formatting | bytes 18874368 | tf_op jit(solution)/shard_map/while/body/eval_jaxpr/reshape | solution.py:67
  205.8 19.1 %scatter_fusion = f32[25,128,128]{2,1,0:T(8,128)S(1)} fusion(f32[25,128,128]{2,1,0:T(8,128)S(1)} %broadcast.274, s32[144]{0:T(256)S(1)} %bitcast.79, f32[144,128,128]{2,1,0:T(8,128)} %copy.29), kind=kCustom, calls=%fused_computation.3.clone.1 | custom fusion | flops 2359296 | bytes 28312128 | tf_op jit(solution)/shard_map/while/body/eval_jaxpr/scatter-add | solution.py:67
  231.3 6.3 gather_fusion.2
  237.6 8.0 %broadcast_multiply_fusion.2 = f32[12,12,128,128]{3,2,1,0:T(8,128)} fusion(f32[12,12]{1,0:T(8,128)S(1)} %fusion.27, bf16[12,12,128,128]{3,2,1,0:T(8,128)(2,1)} %gather_fusion.2, bf16[16,12,128,128]{3,2,1,0:T(8,128)(2,1)} %get-tuple-element.310, s32[]{:T(128)S(6)} %select_n.67), kind=kOutput, calls=%fused_computation.10.clone.1 | convolution fusion | flops 606339072 | bytes 14549572 | tf_op jit(solution)/shard_map/while/body/eval_jaxpr/kcx,klxr->klcr/dot_general | solution.py:62
  245.6 9.6 %copy.29 = f32[144,128,128]{2,1,0:T(8,128)} copy(f32[144,128,128]{1,2,0:T(8,128)} %bitcast.73) | data formatting | bytes 18874368 | tf_op jit(solution)/shard_map/while/body/eval_jaxpr/reshape | solution.py:67
  255.6 19.1 %scatter_fusion = f32[25,128,128]{2,1,0:T(8,128)S(1)} fusion(f32[25,128,128]{2,1,0:T(8,128)S(1)} %broadcast.274, s32[144]{0:T(256)S(1)} %bitcast.79, f32[144,128,128]{2,1,0:T(8,128)} %copy.29), kind=kCustom, calls=%fused_computation.3.clone.1 | custom fusion | flops 2359296 | bytes 28312128 | tf_op jit(solution)/shard_map/while/body/eval_jaxpr/scatter-add | solution.py:67
  281.1 6.3 gather_fusion.2
  287.4 8.0 %broadcast_multiply_fusion.2 = f32[12,12,128,128]{3,2,1,0:T(8,128)} fusion(f32[12,12]{1,0:T(8,128)S(1)} %fusion.27, bf16[12,12,128,128]{3,2,1,0:T(8,128)(2,1)} %gather_fusion.2, bf16[16,12,128,128]{3,2,1,0:T(8,128)(2,1)} %get-tuple-element.310, s32[]{:T(128)S(6)} %select_n.67), kind=kOutput, calls=%fused_computation.10.clone.1 | convolution fusion | flops 606339072 | bytes 14549572 | tf_op jit(solution)/shard_map/while/body/eval_jaxpr/kcx,klxr->klcr/dot_general | solution.py:62
  295.5 9.6 %copy.29 = f32[144,128,128]{2,1,0:T(8,128)} copy(f32[144,128,128]{1,2,0:T(8,128)} %bitcast.73) | data formatting | bytes 18874368 | tf_op jit(solution)/shard_map/while/body/eval_jaxpr/reshape | solution.py:67
  305.5 19.1 %scatter_fusion = f32[25,128,128]{2,1,0:T(8,128)S(1)} fusion(f32[25,128,128]{2,1,0:T(8,128)S(1)} %broadcast.274, s32[144]{0:T(256)S(1)} %bitcast.79, f32[144,128,128]{2,1,0:T(8,128)} %copy.29), kind=kCustom, calls=%fused_computation.3.clone.1 | custom fusion | flops 2359296 | bytes 28312128 | tf_op jit(solution)/shard_map/while/body/eval_jaxpr/scatter-add | solution.py:67
  330.9 6.3 gather_fusion.2
  337.3 8.0 %broadcast_multiply_fusion.2 = f32[12,12,128,128]{3,2,1,0:T(8,128)} fusion(f32[12,12]{1,0:T(8,128)S(1)} %fusion.27, bf16[12,12,128,128]{3,2,1,0:T(8,128)(2,1)} %gather_fusion.2, bf16[16,12,128,128]{3,2,1,0:T(8,128)(2,1)} %get-tuple-element.310, s32[]{:T(128)S(6)} %select_n.67), kind=kOutput, calls=%fused_computation.10.clone.1 | convolution fusion | flops 606339072 | bytes 14549572 | tf_op jit(solution)/shard_map/while/body/eval_jaxpr/kcx,klxr->klcr/dot_general | solution.py:62
  345.3 9.6 %copy.29 = f32[144,128,128]{2,1,0:T(8,128)} copy(f32[144,128,128]{1,2,0:T(8,128)} %bitcast.73) | data formatting | bytes 18874368 | tf_op jit(solution)/shard_map/while/body/eval_jaxpr/reshape | solution.py:67
  355.3 19.1 %scatter_fusion = f32[25,128,128]{2,1,0:T(8,128)S(1)} fusion(f32[25,128,128]{2,1,0:T(8,128)S(1)} %broadcast.274, s32[144]{0:T(256)S(1)} %bitcast.79, f32[144,128,128]{2,1,0:T(8,128)} %copy.29), kind=kCustom, calls=%fused_computation.3.clone.1 | custom fusion | flops 2359296 | bytes 28312128 | tf_op jit(solution)/shard_map/while/body/eval_jaxpr/scatter-add | solution.py:67
  375.8 3.5 copy.27
  379.3 2.7 copy-done
  383.6 3.6 all-to-all-start.1
  387.2 4.8 split.9
  392.0 46.8 %all-to-all-done.1 = f32[8,4,8,16,128]{4,3,2,1,0:T(8,128)S(1)} async-done(((f32[8,4,8,16,128]{4,3,2,1,0:T(8,128)}), f32[8,4,8,16,128]{4,3,2,1,0:T(8,128)S(1)}, u32[]{:S(2)}, u32[]{:S(2)}) %all-to-all-start.1) | async-done | bytes 2097184 | tf_op jit(solution)/shard_map/all_to_all | solution.py:45
  438.8 4.6 all-to-all-start.2
  443.4 99.3 %all-to-all-done.2 = f32[8,4,17,16,128]{4,3,2,1,0:T(8,128)} async-done(((f32[8,4,17,16,128]{4,3,2,1,0:T(8,128)}), f32[8,4,17,16,128]{4,3,2,1,0:T(8,128)}, u32[]{:S(2)}, u32[]{:S(2)}) %all-to-all-start.2) | async-done | bytes 4456480 | tf_op jit(solution)/shard_map/all_to_all | solution.py:45
  542.7 5.6 pad_maximum_fusion
  548.3 94.4 %while.23 = (s32[]{:T(128)}, bf16[32,25,16,128]{3,2,1,0:T(8,128)(2,1)}, s32[32,25,16,128]{3,2,1,0:T(8,128)}, f32[32,25,16,128]{3,2,1,0:T(8,128)}, s32[]{:T(128)}) while((s32[]{:T(128)}, bf16[32,25,16,128]{3,2,1,0:T(8,128)(2,1)}, s32[32,25,16,128]{3,2,1,0:T(8,128)}, f32[32,25,16,128]{3,2,1,0:T(8,128)}, s32[]{:T(128)}) %tuple.56), condition=%wide.region_5.6_spmd, body=%wide.region_3.5_spmd.sunk | while | flops 512002 | bytes 922433 | solution.py:114
  (186 shorter events, 127.4 us)
Async XLA Ops:
  0.0 13.3 %copy-start.1 = (bf16[32,12,16,128]{3,2,1,0:T(8,128)(2,1)S(1)}, bf16[32,12,16,128]{3,2,1,0:T(8,128)(2,1)}, u32[]{:S(2)}) copy-start(bf16[32,12,16,128]{3,2,1,0:T(8,128)(2,1)} %param.8) | copy-start | bytes 4718596
  1.3 8.0 %collective-permute-start = (bf16[6,12,16,128]{3,2,1,0:T(8,128)(2,1)S(1)}, bf16[6,12,16,128]{3,2,1,0:T(8,128)(2,1)S(1)}, u32[]{:S(2)}, u32[]{:S(2)}) collective-permute-start(bf16[6,12,16,128]{3,2,1,0:T(8,128)(2,1)S(1)} %get-tuple-element.184), channel_id=1, source_target_pairs={{0,1},{1,2},{2,3},{3,4},{4,5},{5,6},{6,7},{7,8},{8,9},{9,10},{10,1... | collective-permute-start | bytes 884744 | tf_op jit(solution)/shard_map/ppermute | solution.py:17
  3.2 14.4 %collective-permute-start.1 = (bf16[6,12,16,128]{3,2,1,0:T(8,128)(2,1)S(1)}, bf16[6,12,16,128]{3,2,1,0:T(8,128)(2,1)S(1)}, u32[]{:S(2)}, u32[]{:S(2)}) collective-permute-start(bf16[6,12,16,128]{3,2,1,0:T(8,128)(2,1)S(1)} %get-tuple-element.183), channel_id=1, source_target_pairs={{1,0},{2,1},{3,2},{4,3},{5,4},{6,5},{7,6},{8,7},{9,8},{10,9},{11,1... | collective-permute-start | bytes 884744 | tf_op jit(solution)/shard_map/ppermute | solution.py:18
  19.7 8.6 %copy-start.2 = (s32[1024,12]{0,1:T(8,128)S(1)}, s32[1024,12]{0,1:T(8,128)}, u32[]{:S(2)}) copy-start(s32[1024,12]{0,1:T(8,128)} %param.9) | copy-start | bytes 147460
  19.7 8.9 %copy-start.3 = (s32[1024]{0:T(1024)S(1)}, s32[1024]{0:T(1024)}, u32[]{:S(2)}) copy-start(s32[1024]{0:T(1024)} %param.10) | copy-start | bytes 12292
  19.7 149.4 %all-to-all-start = ((bf16[8,16,12,16,128]{4,3,2,1,0:T(8,128)(2,1)}), bf16[8,16,12,16,128]{4,3,2,1,0:T(8,128)(2,1)}, u32[]{:S(2)}, u32[]{:S(2)}) async-start(bf16[8,16,12,16,128]{4,3,2,1,0:T(8,128)(2,1)} %fusion.11), calls=%async_computation | async-start | bytes 12582912 | tf_op jit(solution)/shard_map/all_to_all | solution.py:94
  379.3 2.7 copy-start
  383.6 55.2 %all-to-all-start.1 = ((f32[8,4,8,16,128]{4,3,2,1,0:T(8,128)}), f32[8,4,8,16,128]{4,3,2,1,0:T(8,128)S(1)}, u32[]{:S(2)}, u32[]{:S(2)}) async-start(f32[8,4,8,16,128]{4,3,2,1,0:T(8,128)} %split.8), calls=%async_computation.1 | async-start | bytes 4194304 | tf_op jit(solution)/shard_map/all_to_all | solution.py:45
  438.8 103.9 %all-to-all-start.2 = ((f32[8,4,17,16,128]{4,3,2,1,0:T(8,128)}), f32[8,4,17,16,128]{4,3,2,1,0:T(8,128)}, u32[]{:S(2)}, u32[]{:S(2)}) async-start(f32[8,4,17,16,128]{4,3,2,1,0:T(8,128)} %split.9), calls=%async_computation.2 | async-start | bytes 8912896 | tf_op jit(solution)/shard_map/all_to_all | solution.py:45
where the time goes:
time: 647 us; the launch traced here: 643 us
  waiting for transfers between devices  289 us (45%)
  other arithmetic  179 us (28%)
  local copies, waits for them, and re-layouts  112 us (17%)
  matrix products  32.2 us (5%)
  starting transfers between devices  22.4 us (3%)
  loops' own time  8.03 us (1%)
    all_to_all x2, waiting for transfers between devices, exchange_in_pieces(): lax.all_to_all(share, axis, split_axis=0, concat_axis=0, tiled=True)  146 us
    all_to_all x1, waiting for transfers between devices, shards(): lax.all_to_all(windows, 'section', split_axis=0, concat_axis=3, tiled=True)  140 us
    scatter-add x4, other arithmetic, expand(): empty.at[target.reshape(-1)]  76.5 us
    dynamic_update_slice x32, other arithmetic, shards(): return lax.map(one_finish, (back, ranks))  56.6 us
    reshape x4, local copies, waits for them, and re-layouts, expand(): weighted.reshape((slots * slots, columns, rows))  38.3 us
    reduce_sum x32, other arithmetic, finish(): totals = jnp.sum(squared, axis=(0, 2), keepdims=True)  37.5 us
    dot_general x4, matrix products, expand(): jnp.einsum('kcx,klxr->klcr', own, firsts, preferred_element_type=jnp.floa...  32.2 us
    gather x4, local copies, waits for them, and re-layouts, expand(): firsts = banded[where_at]  25.3 us
  transfers between devices with their start and end apart: 5, of which 4 were waited for; matrix products, arithmetic and copies ran while one was open for 2% of the time, Pallas kernels for 0%

commit v1 on v0

--- a/solution.py
+++ b/solution.py
@@ -1,3 +1,4 @@
+import functools
 import jax
 import jax.numpy as jnp
 from jax import lax
@@ -5,6 +6,28 @@
 
 W = 6
 TOPK = 256
+
+
+def _part_targets(xs, a_name):
+    work_now = lax.psum(1, a_name)
+    m_next, a_now = (work_now, lax.axis_index(a_name))
+    row_out = xs.shape[0] // m_next
+    z_new = list(xs.shape)
+    z_new[0] = row_out
+    mixed_arr = z_new[3]
+    z_new[3] = mixed_arr * m_next
+    y_new = jnp.zeros(z_new, xs.dtype)
+    to_i = 0
+    while to_i < m_next:
+        even = lax.dynamic_slice_in_dim(xs, (a_now ^ to_i) * row_out, row_out, axis=0)
+        if to_i:
+            even = lax.ppermute(even, a_name, [(dev, dev ^ to_i) for dev in range(m_next)])
+        y_new = lax.dynamic_update_slice_in_dim(y_new, even, (a_now ^ to_i) * mixed_arr, axis=3)
+        to_i += 1
+    return y_new
+
+
+surface_press = functools.partial(_part_targets, a_name="section")
 
 
 def extended(shard, sides, width):
@@ -91,7 +114,7 @@
     start = first_panel + lax.axis_index("section") * share
     sliced = extended(tiles, (("col", 0),), W)
     windows = jnp.stack([sliced[t * share : t * share + share + 2 * W] for t in range(sections)], 0)
-    whole = lax.all_to_all(windows, "section", split_axis=0, concat_axis=3, tiled=True)[0]
+    whole = surface_press(windows)[0]
     win_off = lax.dynamic_slice_in_dim(pad_off, start, share + 2 * W, 0)
     win_cnt = lax.dynamic_slice_in_dim(pad_cnt, start, share + 2 * W, 0)
     loc_off = lax.dynamic_slice_in_dim(offsets, start, share, 0)

time: 647 us -> 658 us (1.017)
  starting transfers between devices: 22.4 us -> 50.2 us
  waiting for transfers between devices: 289 us -> 270 us
    all_to_all x1 -> x0, waiting for transfers between devices: 140 us -> none  [shards(): lax.all_to_all(windows, 'section', split_axis=0, concat_axis=3, tiled=True)]
    ppermute x0 -> x7, waiting for transfers between devices: none -> 118 us  [_part_targets(): lax.ppermute(even, a_name, [(dev, dev ^ to_i) for dev in range(m_next)])]
    ppermute x0 -> x7, starting transfers between devices: none -> 33.1 us  [_part_targets(): lax.ppermute(even, a_name, [(dev, dev ^ to_i) for dev in range(m_next)])]
    all_to_all x1 -> x0, starting transfers between devices: 8.6 us -> none  [shards(): lax.all_to_all(windows, 'section', split_axis=0, concat_axis=3, tiled=True)]
    all_to_all x1 -> x0, local copies, waits for them, and re-layouts: 7.25 us -> none  [shards(): lax.all_to_all(windows, 'section', split_axis=0, concat_axis=3, tiled=True)]
  transfers between devices with their start and end apart: 5 -> 11, of which waited for: 4 -> 9; matrix products, arithmetic and copies ran while one was open for 2% -> 2% of each run, Pallas kernels for 0% -> 0%
where the time goes in v1:
time: 658 us; the launch traced here: 653 us
  waiting for transfers between devices  270 us (41%)
  other arithmetic  179 us (27%)
  local copies, waits for them, and re-layouts  113 us (17%)
  starting transfers between devices  50.2 us (8%)
  matrix products  32.2 us (5%)
  loops' own time  8.16 us (1%)
    all_to_all x2, waiting for transfers between devices, exchange_in_pieces(): lax.all_to_all(share, axis, split_axis=0, concat_axis=0, tiled=True)  150 us
    ppermute x7, waiting for transfers between devices, _part_targets(): lax.ppermute(even, a_name, [(dev, dev ^ to_i) for dev in range(m_next)])  118 us
    scatter-add x4, other arithmetic, expand(): empty.at[target.reshape(-1)]  76.5 us
    dynamic_update_slice x32, other arithmetic, shards(): return lax.map(one_finish, (back, ranks))  56.6 us
    reshape x4, local copies, waits for them, and re-layouts, expand(): weighted.reshape((slots * slots, columns, rows))  38.3 us
    reduce_sum x32, other arithmetic, finish(): totals = jnp.sum(squared, axis=(0, 2), keepdims=True)  37.5 us
    ppermute x7, starting transfers between devices, _part_targets(): lax.ppermute(even, a_name, [(dev, dev ^ to_i) for dev in range(m_next)])  33.1 us
    dot_general x4, matrix products, expand(): jnp.einsum('kcx,klxr->klcr', own, firsts, preferred_element_type=jnp.floa...  32.2 us
  transfers between devices with their start and end apart: 11, of which 9 were waited for; matrix products, arithmetic and copies ran while one was open for 2% of the time, Pallas kernels for 0%

profile of v1, /device:TPU:14, one launch (start us, length us, event | category | flops | bytes accessed | tf_op | source)
XLA Modules:
  0.0 653.3 jit_solution(8443692112354358885)
XLA Ops:
  23.6 6.4 collective-permute-start.5
  33.0 25.3 %collective-permute-done.2 = bf16[1,16,12,16,128]{4,3,2,1,0:T(8,128)(2,1)} collective-permute-done((bf16[1,16,12,16,128]{4,3,2,1,0:T(8,128)(2,1)}, bf16[1,16,12,16,128]{4,3,2,1,0:T(8,128)(2,1)}, u32[]{:S(2)}, u32[]{:S(2)}) %collective-permute-start.2) | collective-permute-done | bytes 786464 | tf_op jit(solution)/shard_map/ppermute | solution.py:24
  58.3 18.6 %collective-permute-start.7 = (bf16[1,16,12,16,128]{4,3,2,1,0:T(8,128)(2,1)S(1)}, bf16[1,16,12,16,128]{4,3,2,1,0:T(8,128)(2,1)S(1)}, u32[]{:S(2)}, u32[]{:S(2)}) collective-permute-start(bf16[1,16,12,16,128]{4,3,2,1,0:T(8,128)(2,1)S(1)} %get-tuple-element.184), channel_id=1, source_target_pairs={{0,192},{32,224},{64,128},{96,160},{128,64},{160,96},{192,0},{224,... | collective-permute-start | bytes 2359304 | tf_op jit(solution)/shard_map/ppermute | solution.py:24
  78.2 11.7 %collective-permute-done.3 = bf16[1,16,12,16,128]{4,3,2,1,0:T(8,128)(2,1)} collective-permute-done((bf16[1,16,12,16,128]{4,3,2,1,0:T(8,128)(2,1)}, bf16[1,16,12,16,128]{4,3,2,1,0:T(8,128)(2,1)}, u32[]{:S(2)}, u32[]{:S(2)}) %collective-permute-start.3) | collective-permute-done | bytes 786464 | tf_op jit(solution)/shard_map/ppermute | solution.py:24
  94.1 45.6 %collective-permute-done.4 = bf16[1,16,12,16,128]{4,3,2,1,0:T(8,128)(2,1)} collective-permute-done((bf16[1,16,12,16,128]{4,3,2,1,0:T(8,128)(2,1)}, bf16[1,16,12,16,128]{4,3,2,1,0:T(8,128)(2,1)}, u32[]{:S(2)}, u32[]{:S(2)}) %collective-permute-start.4) | collective-permute-done | bytes 786464 | tf_op jit(solution)/shard_map/ppermute | solution.py:24
  141.1 16.0 %collective-permute-done.5 = bf16[1,16,12,16,128]{4,3,2,1,0:T(8,128)(2,1)S(1)} collective-permute-done((bf16[1,16,12,16,128]{4,3,2,1,0:T(8,128)(2,1)S(1)}, bf16[1,16,12,16,128]{4,3,2,1,0:T(8,128)(2,1)S(1)}, u32[]{:S(2)}, u32[]{:S(2)}) %collective-permute-start.5) | collective-permute-done | bytes 786464 | tf_op jit(solution)/shard_map/ppermute | solution.py:24
  157.3 5.0 collective-permute-done.6
  162.8 14.5 %collective-permute-done.8 = bf16[1,16,12,16,128]{4,3,2,1,0:T(8,128)(2,1)S(1)} collective-permute-done((bf16[1,16,12,16,128]{4,3,2,1,0:T(8,128)(2,1)S(1)}, bf16[1,16,12,16,128]{4,3,2,1,0:T(8,128)(2,1)S(1)}, u32[]{:S(2)}, u32[]{:S(2)}) %collective-permute-start.8) | collective-permute-done | bytes 786464 | tf_op jit(solution)/shard_map/ppermute | solution.py:24
  180.2 199.6 %while.22 = (s32[]{:T(128)}, f32[4,25,128,128]{3,2,1,0:T(8,128)}, s32[4,12]{1,0:T(4,128)S(1)}, s32[4]{0:T(128)S(1)}, s32[16,12]{1,0:T(8,128)S(1)}, /*index=5*/bf...) while((s32[]{:T(128)}, f32[4,25,128,128]{3,2,1,0:T(8,128)}, ...), condition=%wide.region_2.3_spmd, body=%wide.region_0.2_spmd.sunk | while | flops 608701376 | bytes 76102056 | solution.py:130
  185.2 6.3 gather_fusion.2
  191.6 8.0 %broadcast_multiply_fusion.2 = f32[12,12,128,128]{3,2,1,0:T(8,128)} fusion(f32[12,12]{1,0:T(8,128)S(1)} %fusion.27, bf16[12,12,128,128]{3,2,1,0:T(8,128)(2,1)} %gather_fusion.2, bf16[16,12,128,128]{3,2,1,0:T(8,128)(2,1)} %get-tuple-element.317, s32[]{:T(128)S(6)} %select_n.131), kind=kOutput, calls=%fused_computation.10.clone.1 | convolution fusion | flops 606339072 | bytes 14549572 | tf_op jit(solution)/shard_map/while/body/eval_jaxpr/kcx,klxr->klcr/dot_general | solution.py:85
  199.6 9.6 %copy.26 = f32[144,128,128]{2,1,0:T(8,128)} copy(f32[144,128,128]{1,2,0:T(8,128)} %bitcast.85) | data formatting | bytes 18874368 | tf_op jit(solution)/shard_map/while/body/eval_jaxpr/reshape | solution.py:90
  209.6 19.1 %scatter_fusion = f32[25,128,128]{2,1,0:T(8,128)S(1)} fusion(f32[25,128,128]{2,1,0:T(8,128)S(1)} %broadcast.276, s32[144]{0:T(256)S(1)} %bitcast.90, f32[144,128,128]{2,1,0:T(8,128)} %copy.26), kind=kCustom, calls=%fused_computation.3.clone.1 | custom fusion | flops 2359296 | bytes 28312128 | tf_op jit(solution)/shard_map/while/body/eval_jaxpr/scatter-add | solution.py:90
  235.1 6.3 gather_fusion.2
  241.4 8.0 %broadcast_multiply_fusion.2 = f32[12,12,128,128]{3,2,1,0:T(8,128)} fusion(f32[12,12]{1,0:T(8,128)S(1)} %fusion.27, bf16[12,12,128,128]{3,2,1,0:T(8,128)(2,1)} %gather_fusion.2, bf16[16,12,128,128]{3,2,1,0:T(8,128)(2,1)} %get-tuple-element.317, s32[]{:T(128)S(6)} %select_n.131), kind=kOutput, calls=%fused_computation.10.clone.1 | convolution fusion | flops 606339072 | bytes 14549572 | tf_op jit(solution)/shard_map/while/body/eval_jaxpr/kcx,klxr->klcr/dot_general | solution.py:85
  249.4 9.6 %copy.26 = f32[144,128,128]{2,1,0:T(8,128)} copy(f32[144,128,128]{1,2,0:T(8,128)} %bitcast.85) | data formatting | bytes 18874368 | tf_op jit(solution)/shard_map/while/body/eval_jaxpr/reshape | solution.py:90
  259.5 19.1 %scatter_fusion = f32[25,128,128]{2,1,0:T(8,128)S(1)} fusion(f32[25,128,128]{2,1,0:T(8,128)S(1)} %broadcast.276, s32[144]{0:T(256)S(1)} %bitcast.90, f32[144,128,128]{2,1,0:T(8,128)} %copy.26), kind=kCustom, calls=%fused_computation.3.clone.1 | custom fusion | flops 2359296 | bytes 28312128 | tf_op jit(solution)/shard_map/while/body/eval_jaxpr/scatter-add | solution.py:90
  284.9 6.3 gather_fusion.2
  291.3 8.0 %broadcast_multiply_fusion.2 = f32[12,12,128,128]{3,2,1,0:T(8,128)} fusion(f32[12,12]{1,0:T(8,128)S(1)} %fusion.27, bf16[12,12,128,128]{3,2,1,0:T(8,128)(2,1)} %gather_fusion.2, bf16[16,12,128,128]{3,2,1,0:T(8,128)(2,1)} %get-tuple-element.317, s32[]{:T(128)S(6)} %select_n.131), kind=kOutput, calls=%fused_computation.10.clone.1 | convolution fusion | flops 606339072 | bytes 14549572 | tf_op jit(solution)/shard_map/while/body/eval_jaxpr/kcx,klxr->klcr/dot_general | solution.py:85
  299.3 9.6 %copy.26 = f32[144,128,128]{2,1,0:T(8,128)} copy(f32[144,128,128]{1,2,0:T(8,128)} %bitcast.85) | data formatting | bytes 18874368 | tf_op jit(solution)/shard_map/while/body/eval_jaxpr/reshape | solution.py:90
  309.3 19.1 %scatter_fusion = f32[25,128,128]{2,1,0:T(8,128)S(1)} fusion(f32[25,128,128]{2,1,0:T(8,128)S(1)} %broadcast.276, s32[144]{0:T(256)S(1)} %bitcast.90, f32[144,128,128]{2,1,0:T(8,128)} %copy.26), kind=kCustom, calls=%fused_computation.3.clone.1 | custom fusion | flops 2359296 | bytes 28312128 | tf_op jit(solution)/shard_map/while/body/eval_jaxpr/scatter-add | solution.py:90
  334.8 6.3 gather_fusion.2
  341.2 8.0 %broadcast_multiply_fusion.2 = f32[12,12,128,128]{3,2,1,0:T(8,128)} fusion(f32[12,12]{1,0:T(8,128)S(1)} %fusion.27, bf16[12,12,128,128]{3,2,1,0:T(8,128)(2,1)} %gather_fusion.2, bf16[16,12,128,128]{3,2,1,0:T(8,128)(2,1)} %get-tuple-element.317, s32[]{:T(128)S(6)} %select_n.131), kind=kOutput, calls=%fused_computation.10.clone.1 | convolution fusion | flops 606339072 | bytes 14549572 | tf_op jit(solution)/shard_map/while/body/eval_jaxpr/kcx,klxr->klcr/dot_general | solution.py:85
  349.2 9.6 %copy.26 = f32[144,128,128]{2,1,0:T(8,128)} copy(f32[144,128,128]{1,2,0:T(8,128)} %bitcast.85) | data formatting | bytes 18874368 | tf_op jit(solution)/shard_map/while/body/eval_jaxpr/reshape | solution.py:90
  359.2 19.1 %scatter_fusion = f32[25,128,128]{2,1,0:T(8,128)S(1)} fusion(f32[25,128,128]{2,1,0:T(8,128)S(1)} %broadcast.276, s32[144]{0:T(256)S(1)} %bitcast.90, f32[144,128,128]{2,1,0:T(8,128)} %copy.26), kind=kCustom, calls=%fused_computation.3.clone.1 | custom fusion | flops 2359296 | bytes 28312128 | tf_op jit(solution)/shard_map/while/body/eval_jaxpr/scatter-add | solution.py:90
  387.5 6.9 %all-to-all-start = ((f32[8,4,8,16,128]{4,3,2,1,0:T(8,128)}), f32[8,4,8,16,128]{4,3,2,1,0:T(8,128)S(1)}, u32[]{:S(2)}, u32[]{:S(2)}) async-start(f32[8,4,8,16,128]{4,3,2,1,0:T(8,128)} %split.8), calls=%async_computation | async-start | bytes 4194304 | tf_op jit(solution)/shard_map/all_to_all | solution.py:68
  394.4 4.8 split.9
  399.2 47.2 %all-to-all-done = f32[8,4,8,16,128]{4,3,2,1,0:T(8,128)S(1)} async-done(((f32[8,4,8,16,128]{4,3,2,1,0:T(8,128)}), f32[8,4,8,16,128]{4,3,2,1,0:T(8,128)S(1)}, u32[]{:S(2)}, u32[]{:S(2)}) %all-to-all-start) | async-done | bytes 2097184 | tf_op jit(solution)/shard_map/all_to_all | solution.py:68
  446.4 4.6 all-to-all-start.1
  451.0 102.4 %all-to-all-done.1 = f32[8,4,17,16,128]{4,3,2,1,0:T(8,128)} async-done(((f32[8,4,17,16,128]{4,3,2,1,0:T(8,128)}), f32[8,4,17,16,128]{4,3,2,1,0:T(8,128)}, u32[]{:S(2)}, u32[]{:S(2)}) %all-to-all-start.1) | async-done | bytes 4456480 | tf_op jit(solution)/shard_map/all_to_all | solution.py:68
  553.4 5.6 pad_maximum_fusion
  558.9 94.4 %while.23 = (s32[]{:T(128)}, bf16[32,25,16,128]{3,2,1,0:T(8,128)(2,1)}, s32[32,25,16,128]{3,2,1,0:T(8,128)}, f32[32,25,16,128]{3,2,1,0:T(8,128)}, s32[]{:T(128)}) while((s32[]{:T(128)}, bf16[32,25,16,128]{3,2,1,0:T(8,128)(2,1)}, s32[32,25,16,128]{3,2,1,0:T(8,128)}, f32[32,25,16,128]{3,2,1,0:T(8,128)}, s32[]{:T(128)}) %tuple.62), condition=%wide.region_5.6_spmd, body=%wide.region_3.5_spmd.sunk | while | flops 512002 | bytes 922433 | solution.py:137
  (211 shorter events, 158.2 us)
Async XLA Ops:
  0.0 11.6 %copy-start.2 = (bf16[32,12,16,128]{3,2,1,0:T(8,128)(2,1)S(1)}, bf16[32,12,16,128]{3,2,1,0:T(8,128)(2,1)}, u32[]{:S(2)}) copy-start(bf16[32,12,16,128]{3,2,1,0:T(8,128)(2,1)} %param.8) | copy-start | bytes 4718596
  1.3 8.0 %collective-permute-start = (bf16[6,12,16,128]{3,2,1,0:T(8,128)(2,1)S(1)}, bf16[6,12,16,128]{3,2,1,0:T(8,128)(2,1)S(1)}, u32[]{:S(2)}, u32[]{:S(2)}) collective-permute-start(bf16[6,12,16,128]{3,2,1,0:T(8,128)(2,1)S(1)} %get-tuple-element.191), channel_id=1, source_target_pairs={{0,1},{1,2},{2,3},{3,4},{4,5},{5,6},{6,7},{7,8},{8,9},{9,10},{10,1... | collective-permute-start | bytes 884744 | tf_op jit(solution)/shard_map/ppermute | solution.py:40
  3.2 9.2 %collective-permute-start.1 = (bf16[6,12,16,128]{3,2,1,0:T(8,128)(2,1)S(1)}, bf16[6,12,16,128]{3,2,1,0:T(8,128)(2,1)S(1)}, u32[]{:S(2)}, u32[]{:S(2)}) collective-permute-start(bf16[6,12,16,128]{3,2,1,0:T(8,128)(2,1)S(1)} %get-tuple-element.190), channel_id=1, source_target_pairs={{1,0},{2,1},{3,2},{4,3},{5,4},{6,5},{7,6},{8,7},{9,8},{10,9},{11,1... | collective-permute-start | bytes 884744 | tf_op jit(solution)/shard_map/ppermute | solution.py:41
  12.6 10.2 %copy-start.4 = (s32[1024,12]{0,1:T(8,128)S(1)}, s32[1024,12]{0,1:T(8,128)}, u32[]{:S(2)}) copy-start(s32[1024,12]{0,1:T(8,128)} %param.9) | copy-start | bytes 147460
  12.7 10.6 %copy-start.5 = (s32[1024]{0:T(1024)S(1)}, s32[1024]{0:T(1024)}, u32[]{:S(2)}) copy-start(s32[1024]{0:T(1024)} %param.10) | copy-start | bytes 12292
  12.9 2.7 copy-start.3
  17.7 40.6 %collective-permute-start.2 = (bf16[1,16,12,16,128]{4,3,2,1,0:T(8,128)(2,1)}, bf16[1,16,12,16,128]{4,3,2,1,0:T(8,128)(2,1)}, u32[]{:S(2)}, u32[]{:S(2)}) collective-permute-start(bf16[1,16,12,16,128]{4,3,2,1,0:T(8,128)(2,1)} %get-tuple-element.189), channel_id=1, source_target_pairs={{0,32},{32,0},{64,96},{96,64},{128,160},{160,128},{192,224},{224,1... | collective-permute-start | bytes 2359304 | tf_op jit(solution)/shard_map/ppermute | solution.py:24
  19.6 70.3 %collective-permute-start.3 = (bf16[1,16,12,16,128]{4,3,2,1,0:T(8,128)(2,1)}, bf16[1,16,12,16,128]{4,3,2,1,0:T(8,128)(2,1)}, u32[]{:S(2)}, u32[]{:S(2)}) collective-permute-start(bf16[1,16,12,16,128]{4,3,2,1,0:T(8,128)(2,1)} %get-tuple-element.188), channel_id=1, source_target_pairs={{0,64},{32,96},{64,0},{96,32},{128,192},{160,224},{192,128},{224,1... | collective-permute-start | bytes 2359304 | tf_op jit(solution)/shard_map/ppermute | solution.py:24
  23.0 116.7 %collective-permute-start.4 = (bf16[1,16,12,16,128]{4,3,2,1,0:T(8,128)(2,1)}, bf16[1,16,12,16,128]{4,3,2,1,0:T(8,128)(2,1)}, u32[]{:S(2)}, u32[]{:S(2)}) collective-permute-start(bf16[1,16,12,16,128]{4,3,2,1,0:T(8,128)(2,1)} %get-tuple-element.187), channel_id=1, source_target_pairs={{0,96},{32,64},{64,32},{96,0},{128,224},{160,192},{192,160},{224,1... | collective-permute-start | bytes 2359304 | tf_op jit(solution)/shard_map/ppermute | solution.py:24
  23.6 133.4 %collective-permute-start.5 = (bf16[1,16,12,16,128]{4,3,2,1,0:T(8,128)(2,1)S(1)}, bf16[1,16,12,16,128]{4,3,2,1,0:T(8,128)(2,1)S(1)}, u32[]{:S(2)}, u32[]{:S(2)}) collective-permute-start(bf16[1,16,12,16,128]{4,3,2,1,0:T(8,128)(2,1)S(1)} %get-tuple-element.186), channel_id=1, source_target_pairs={{0,128},{32,160},{64,192},{96,224},{128,0},{160,32},{192,64},{224,... | collective-permute-start | bytes 2359304 | tf_op jit(solution)/shard_map/ppermute | solution.py:24
  30.0 132.3 %collective-permute-start.6 = (bf16[1,16,12,16,128]{4,3,2,1,0:T(8,128)(2,1)S(1)}, bf16[1,16,12,16,128]{4,3,2,1,0:T(8,128)(2,1)S(1)}, u32[]{:S(2)}, u32[]{:S(2)}) collective-permute-start(bf16[1,16,12,16,128]{4,3,2,1,0:T(8,128)(2,1)S(1)} %get-tuple-element.185), channel_id=1, source_target_pairs={{0,160},{32,128},{64,224},{96,192},{128,32},{160,0},{192,96},{224,... | collective-permute-start | bytes 2359304 | tf_op jit(solution)/shard_map/ppermute | solution.py:24
  58.3 104.3 %collective-permute-start.7 = (bf16[1,16,12,16,128]{4,3,2,1,0:T(8,128)(2,1)S(1)}, bf16[1,16,12,16,128]{4,3,2,1,0:T(8,128)(2,1)S(1)}, u32[]{:S(2)}, u32[]{:S(2)}) collective-permute-start(bf16[1,16,12,16,128]{4,3,2,1,0:T(8,128)(2,1)S(1)} %get-tuple-element.184), channel_id=1, source_target_pairs={{0,192},{32,224},{64,128},{96,160},{128,64},{160,96},{192,0},{224,... | collective-permute-start | bytes 2359304 | tf_op jit(solution)/shard_map/ppermute | solution.py:24
  89.9 87.4 %collective-permute-start.8 = (bf16[1,16,12,16,128]{4,3,2,1,0:T(8,128)(2,1)S(1)}, bf16[1,16,12,16,128]{4,3,2,1,0:T(8,128)(2,1)S(1)}, u32[]{:S(2)}, u32[]{:S(2)}) collective-permute-start(bf16[1,16,12,16,128]{4,3,2,1,0:T(8,128)(2,1)S(1)} %get-tuple-element.183), channel_id=1, source_target_pairs={{0,224},{32,192},{64,160},{96,128},{128,96},{160,64},{192,32},{224... | collective-permute-start | bytes 2359304 | tf_op jit(solution)/shard_map/ppermute | solution.py:24
  177.5 2.7 copy-start
  383.2 2.7 copy-start.1
  387.5 58.9 %all-to-all-start = ((f32[8,4,8,16,128]{4,3,2,1,0:T(8,128)}), f32[8,4,8,16,128]{4,3,2,1,0:T(8,128)S(1)}, u32[]{:S(2)}, u32[]{:S(2)}) async-start(f32[8,4,8,16,128]{4,3,2,1,0:T(8,128)} %split.8), calls=%async_computation | async-start | bytes 4194304 | tf_op jit(solution)/shard_map/all_to_all | solution.py:68
  446.4 107.0 %all-to-all-start.1 = ((f32[8,4,17,16,128]{4,3,2,1,0:T(8,128)}), f32[8,4,17,16,128]{4,3,2,1,0:T(8,128)}, u32[]{:S(2)}, u32[]{:S(2)}) async-start(f32[8,4,17,16,128]{4,3,2,1,0:T(8,128)} %split.9), calls=%async_computation.1 | async-start | bytes 8912896 | tf_op jit(solution)/shard_map/all_to_all | solution.py:68
